TPU v7x, 128 devices: a whole 4x4x4 slice. The times are simulated.
128 devices in a mesh: blk: 32 (over y, x, core), rep: 4 (over z).
Axes of the slice: x: 4, y: 4, z: 4, core: 2. Of those that a mesh axis runs over, the one named last changes fastest.
Arguments:
- anchors: float32 [3, 81920], P(None, ('blk', 'rep')), may hold values from -1 to 1
- directions: float32 [3, 81920], P(None, ('blk', 'rep')), may hold values from -4 to 4
- app_ids: int32 [81920], P(('blk', 'rep')), may hold values from 0 to 8191
- block_ids: int32 [640, 3], P(('blk', 'rep')), may hold values from 0 to 31, as said below
- color_grad: float32 [3, 81920], P(None, ('blk', 'rep')), may hold values from -6 to 6
- block_centers: float32 [3, 32], P(None, 'blk'), may hold values from -1 to 1
- pos_weight: bfloat16 [32, 256, 63], P('blk'), may hold values from -1 to 1
- trunk_weight: bfloat16 [32, 2, 256, 256], P('blk'), may hold values from -0.5 to 0.5
- density_weight: bfloat16 [32, 256], P('blk'), may hold values from -0.5 to 0.5
- feature_weight: bfloat16 [32, 128, 256], P('blk'), may hold values from -0.5 to 0.5
- view_weight: bfloat16 [32, 128, 27], P('blk'), may hold values from -1.25 to 1.25
- code_weight: bfloat16 [32, 128, 32], P('blk'), may hold values from -1 to 1
- radiance_weight: bfloat16 [32, 3, 128], P('blk'), may hold values from -0.75 to 0.75
- code_table: bfloat16 [32, 32, 8192], P('blk'), may hold values from -5 to 5
Outputs:
- colors: float32 [3, 81920], P(None, ('blk', 'rep'))
- grad_pos_weight: float32 [32, 256, 63], P('blk')
- grad_trunk_weight: float32 [32, 2, 256, 256], P('blk')
- grad_density_weight: float32 [32, 256], P('blk')
- grad_feature_weight: float32 [32, 128, 256], P('blk')
- grad_view_weight: float32 [32, 128, 27], P('blk')
- grad_code_weight: float32 [32, 128, 32], P('blk')
- grad_radiance_weight: float32 [32, 3, 128], P('blk')
- grad_code_table: float32 [32, 32, 8192], P('blk')
Inputs may be any that keep to these rules, and one draw needn't show every extreme that they name: `block_ids`: each tile names three different blocks; the tiles of one device never name the same block twice; among the devices that share an index along rep, every block is named by at most 30 tiles, and some block by exactly 30 tiles.
All inputs are finite; a program needn't handle non-finite values.
Results may differ from a plain program's by a relative error of at most 0.015.
Values sent between devices are 32-bit elements; how exact they have to be, the bound alone decides.
A program may use at most 64 MiB of HBM per device.

v0:
```python
import numpy as np

import jax
import jax.numpy as jnp
from jax import lax
from jax.experimental import pallas as pl
from jax.experimental.pallas import tpu as pltpu
from jax.sharding import PartitionSpec as P

TILE = 128
SAMPLES = 4
SLOTS = 32
LANES = SAMPLES * TILE
HID = 256
CHID = 128
PC = 96
VC = 48
E = 32
RC = VC + E
LO = 256
SPACING = 0.5
LOSS_SCALE = 0.03125
DEEP = 3
PARTS_F = 4
PARTS_B = 4

R_H1 = PC
R_H2 = R_H1 + HID
R_H3 = R_H2 + HID
R_S = R_H3 + HID
R_END = R_S + CHID
GATHER_AFTER = R_H2

G_T1 = 0
G_T2 = 256
G_FEAT = 512
G_TAB = 640
G_POS = 1664
G_VIEW = 1728
G_CODE = 1760
G_RAD = 1728
G_DEN = 1744
G_ROWS = 1792


def code_places(levels, half):
    raw = list(range(3))
    sines, cosines = [], []
    for level in range(levels):
        for c in range(3):
            row = (level // half) * 3 + c
            group = 2 * (level % half)
            sines.append(8 * (1 + group) + row)
            cosines.append(8 * (2 + group) + row)
    return raw + sines + cosines


def selection(places, width):
    out = np.zeros((len(places), width), np.float32)
    out[np.arange(len(places)), places] = 1.0
    return out


POS_SELECT = selection(code_places(10, 5), PC)
VIEW_SELECT = selection(code_places(4, 2), VC)


def mm(a, b):
    return lax.dot_general(a, b, (((1,), (0,)), ((), ())), preferred_element_type=jnp.float32)


def mm_nt(a, b):
    return lax.dot_general(a, b, (((1,), (1,)), ((), ())), preferred_element_type=jnp.float32)


def mm_tn(a, b):
    return lax.dot_general(a, b, (((0,), (0,)), ((), ())), preferred_element_type=jnp.float32)


def softplus(v):
    return jnp.maximum(v, jnp.log(1.0 + jnp.exp(jnp.minimum(v, 80.0))))


def row_iota(rows, lanes):
    return lax.broadcasted_iota(jnp.int32, (rows, lanes), 0)


def ray_rows(ray, row):
    o8 = jnp.where(row < 3, ray, jnp.where(row < 6, pltpu.roll(ray, 3, 0), 0.0))
    d8 = jnp.where(row < 3, pltpu.roll(ray, 5, 0), jnp.where(row < 6, ray, 0.0))
    return o8, d8


def center_rows(center_ref, row):
    third = jnp.where(row >= 3, row - 3, row)
    return jnp.where(
        third == 0,
        center_ref[0, 0],
        jnp.where(third == 1, center_ref[0, 1], jnp.where(third == 2, center_ref[0, 2], 0.0)),
    )


def sine_cosine(x):
    turns = jnp.round(x * 0.6366197723675814)
    r = x - turns * 1.5703125
    r = r - turns * 4.837512969970703e-4
    r = r - turns * 7.549789948768648e-8
    q = turns.astype(jnp.int32)
    z = r * r
    sine = r + r * z * (-1.6666654611e-1 + z * (8.3321608736e-3 - z * 1.9515295891e-4))
    cosine = 1.0 - 0.5 * z + z * z * (
        4.166664568298827e-2 + z * (-1.388731625493765e-3 + z * 2.443315711809948e-5)
    )
    odd = (q & 1) == 1
    first = jnp.where(odd, cosine, sine)
    second = jnp.where(odd, sine, cosine)
    return (
        jnp.where((q & 2) == 2, -first, first),
        jnp.where(((q + 1) & 2) == 2, -second, second),
    )


def code_groups(values, doublings):
    groups = [values]
    sine, cosine = sine_cosine(values)
    for step in range(doublings):
        groups += [sine, cosine]
        if step + 1 < doublings:
            sine, cosine = 2.0 * sine * cosine, (cosine - sine) * (cosine + sine)
    groups.append(jnp.zeros_like(values))
    return jnp.concatenate(groups, 0).astype(jnp.bfloat16)


def halves(x):
    return x[:, :TILE], x[:, TILE:]


def over_samples(x):
    return [
        jnp.concatenate([x[:, s * TILE : (s + 1) * TILE], x[:, LANES + s * TILE : LANES + (s + 1) * TILE]], 1)
        for s in range(SAMPLES)
    ]


def by_samples(pieces):
    return jnp.concatenate([halves(p)[h] for h in range(2) for p in pieces], 1)


def composite(small, o8, c8, row):
    density = over_samples(softplus(small))
    rad = over_samples(1.0 / (1.0 + jnp.exp(-small)))
    off = o8 - c8
    off2 = jnp.sum(jnp.where(row < 3, off * off, 0.0), 0, keepdims=True)
    inv = 1.0 / (1.0 + off2)
    depth = jnp.zeros((1, 2 * TILE), jnp.float32)
    before = jnp.ones((1, 2 * TILE), jnp.float32)
    weights, after = [], []
    for s in range(SAMPLES):
        u = density[s][3:4] * SPACING
        weights.append(before * (1.0 - jnp.exp(-u)))
        depth = depth + u
        before = jnp.exp(-depth)
        after.append(before)
    color = sum(w * r for w, r in zip(weights, rad))
    opacity = sum(weights)
    return rad, weights, after, color, (0.1 + opacity) * inv, inv


def list_live(live_ref, slots):
    total = jnp.int32(0)
    for s in range(SLOTS):
        slots[total] = jnp.int32(s)
        total = total + (live_ref[s] > 0).astype(jnp.int32)

    @pl.when(total % 2 == 1)
    def _():
        slots[total] = slots[total - 1]

    return total, (total + 1) // 2


def pair_copies(buf, saved_ref, sem, j, out):
    slot = lax.rem(j, DEEP)
    copies = []
    for n, (lo, hi) in enumerate(((0, 256), (256, 512), (512, 752), (752, R_END))):
        near, far = buf.at[slot, lo:hi], saved_ref.at[j, lo:hi]
        src, dst = (near, far) if out else (far, near)
        copies.append(pltpu.make_async_copy(src, dst, sem.at[slot, n]))
    return copies


def hot_lanes(ids):
    lo, hi = ids & (LO - 1), ids >> 8
    return (row_iota(LO, 2 * TILE) == lo).astype(jnp.float32).astype(jnp.bfloat16), hi


def lane_parts(parts):
    width = 2 * LANES // parts
    return [slice(p * width, (p + 1) * width) for p in range(parts)]


def forward_kernel(
    live_ref, center_ref, rays_ref, pos_ref, trunk_ref, density_ref, feature_ref, view_ref,
    code_ref, radiance_ref, table_ref, pos_select_ref, view_select_ref,
    part_ref, saved_ref, raycode_ref, small_ref,
    wp, wfd, wray, wrad, tab, buf, slots, sem,
):
    row = row_iota(8, 2 * TILE)
    c8 = center_rows(center_ref, row)
    wp[...] = mm_tn(pos_select_ref[...], pos_ref[0]).T.astype(jnp.bfloat16)
    wray[...] = jnp.concatenate(
        [mm_tn(view_select_ref[...], view_ref[0]), code_ref[0].astype(jnp.float32)], 0
    ).T.astype(jnp.bfloat16)
    wfd[:CHID, :] = feature_ref[0]
    row16 = row_iota(16, HID)
    wfd[CHID:, :] = jnp.where(row16 == 3, density_ref[...].astype(jnp.float32), 0.0).astype(jnp.bfloat16)
    wrad[...] = jnp.concatenate(
        [radiance_ref[0].astype(jnp.float32), jnp.zeros((5, CHID), jnp.float32)], 0
    ).astype(jnp.bfloat16)
    for h in range(SLOTS):
        tab[h * E : (h + 1) * E, :] = table_ref[0, :, h * LO : (h + 1) * LO]
    pos_scale = jnp.where(row < 3, 1.0, 32.0)
    view_scale = jnp.where(row < 3, 1.0, 4.0)
    total, pairs = list_live(live_ref, slots)

    def finish_pair(j):
        s0, s1 = slots[2 * j], slots[2 * j + 1]
        o8, _ = ray_rows(jnp.concatenate([rays_ref[s0], rays_ref[s1]], 1), row)
        _, _, _, color, share, _ = composite(small_ref[j], o8, c8, row)
        first, second = halves(jnp.where(row < 3, color * share, share)[:4])
        part_ref[s0] = first
        part_ref[s1] = second

    def pair(j, carry):
        @pl.when(j >= DEEP)
        def _():
            for copy in pair_copies(buf, saved_ref, sem, j - DEEP, True):
                copy.wait()

        out = buf.at[lax.rem(j, DEEP)]
        s0, s1 = slots[2 * j], slots[2 * j + 1]
        ray = jnp.concatenate([rays_ref[s0], rays_ref[s1]], 1)
        o8, d8 = ray_rows(ray, row)
        points = by_samples(
            [(o8 + (t + 0.5) * SPACING * d8 - c8) * pos_scale for t in range(SAMPLES)]
        )
        out[:PC, :] = code_groups(points, 5)
        finish_pair(jnp.maximum(j - 1, 0))
        lanes = lane_parts(PARTS_F)
        for w, lo, mid, hi_row in (
            (wp, 0, R_H1, R_H2), (trunk_ref.at[0, 0], R_H1, R_H2, R_H3), (trunk_ref.at[0, 1], R_H2, R_H3, R_S)
        ):
            for part in lanes:
                out[mid:hi_row, part] = softplus(mm(w[...], out[lo:mid, part])).astype(jnp.bfloat16)
            if mid == GATHER_AFTER:
                hot, hi = hot_lanes(ray[6:7].astype(jnp.int32))
                rows = mm(tab[...], hot)
                picks = [rows[h * E : (h + 1) * E] for h in range(SLOTS)]
                for bit in range(5):
                    on = ((hi >> bit) & 1) == 1
                    picks = [jnp.where(on, b, a) for a, b in zip(picks[::2], picks[1::2])]
                app = picks[0]
                raycode = jnp.concatenate([code_groups(d8 * view_scale, 2), app.astype(jnp.bfloat16)], 0)
                raycode_ref[j] = raycode
                per_ray = mm(wray[...], raycode)
        ray_lanes = by_samples([per_ray] * SAMPLES)
        small = []
        for part in lanes:
            both = mm(wfd[...], out[R_H3:R_S, part])
            shaded = softplus(both[:CHID] + ray_lanes[:, part]).astype(jnp.bfloat16)
            out[R_S:R_END, part] = shaded
            logits = mm(wrad[...], shaded)
            small.append(jnp.where(row_iota(8, logits.shape[1]) == 3, both[CHID : CHID + 8], logits))
        small = jnp.concatenate(small, 1)
        small_ref[j] = small
        for copy in pair_copies(buf, saved_ref, sem, j, True):
            copy.start()
        return carry

    small_ref[0] = jnp.zeros_like(small_ref[0])
    lax.fori_loop(0, pairs, pair, jnp.int32(0))

    @pl.when(pairs > 0)
    def _():
        finish_pair(pairs - 1)

    def drain(j, carry):
        for copy in pair_copies(buf, saved_ref, sem, j, True):
            copy.wait()
        return carry

    lax.fori_loop(jnp.maximum(pairs - DEEP, 0), pairs, drain, jnp.int32(0))


def backward_kernel(
    live_ref, center_ref, rays_ref, cot_ref, saved_ref, raycode_ref, small_ref, trunk_ref,
    density_ref, feature_ref, code_ref, radiance_ref, pos_select_ref, view_select_ref,
    g_ref,
    t1, t2, fdt, radt, dz0, dz1, dz2, dz3, d_logits, g_pos, g_ray, g_rad, buf, slots, sem,
):
    total, pairs = list_live(live_ref, slots)

    def fetch(j, carry):
        for copy in pair_copies(buf, saved_ref, sem, j, False):
            copy.start()
        return carry

    lax.fori_loop(0, jnp.minimum(pairs, DEEP - 1), fetch, jnp.int32(0))
    row = row_iota(8, 2 * TILE)
    lane = lax.broadcasted_iota(jnp.int32, (1, 2 * TILE), 1)
    c8 = center_rows(center_ref, row)

    def flip(x):
        return x.astype(jnp.float32).T.astype(jnp.bfloat16)

    t1[...] = flip(trunk_ref[0, 0])
    t2[...] = flip(trunk_ref[0, 1])
    fdt[:, :CHID] = flip(feature_ref[0])
    row16 = row_iota(16, HID)
    fdt[:, CHID:] = jnp.where(row16 == 3, density_ref[...].astype(jnp.float32), 0.0).T.astype(jnp.bfloat16)
    radt[...] = jnp.concatenate(
        [radiance_ref[0].astype(jnp.float32), jnp.zeros((13, CHID), jnp.float32)], 0
    ).T.astype(jnp.bfloat16)
    g_ref[...] = jnp.zeros_like(g_ref)
    g_pos[...] = jnp.zeros_like(g_pos)
    g_ray[...] = jnp.zeros_like(g_ray)
    g_rad[...] = jnp.zeros_like(g_rad)

    def start_pair(j):
        s0, s1 = slots[2 * j], slots[2 * j + 1]
        ray = jnp.concatenate([rays_ref[s0], rays_ref[s1]], 1)
        o8, _ = ray_rows(ray, row)
        small = small_ref[j]
        rad, weights, after, color, share, inv = composite(small, o8, c8, row)
        cot = jnp.concatenate([cot_ref[s0], cot_ref[s1]], 1)
        cot = jnp.where((lane < TILE) | (2 * j + 1 < total), cot, 0.0)
        cot = jnp.concatenate([cot, jnp.zeros_like(cot)], 0)
        d_share = jnp.sum(
            jnp.where(row < 3, cot * color, jnp.where(row == 3, cot, 0.0)), 0, keepdims=True
        )
        d_color = jnp.where(row < 3, cot * share, 0.0)
        d_opacity = d_share * inv
        sig = rad
        later = jnp.zeros((1, 2 * TILE), jnp.float32)
        pieces = [None] * SAMPLES
        for t in reversed(range(SAMPLES)):
            d_w = jnp.sum(d_color * rad[t], 0, keepdims=True) + d_opacity
            d_u = d_w * after[t] - later
            later = later + d_w * weights[t]
            d_logit = d_color * weights[t] * rad[t] * (1.0 - rad[t])
            pieces[t] = jnp.where(
                row < 3, d_logit, jnp.where(row == 3, d_u * SPACING * sig[t], 0.0)
            )
        d_small = by_samples(pieces)
        d_logits[...] = jnp.concatenate([d_small, jnp.zeros_like(d_small)], 0).astype(jnp.bfloat16)

    @pl.when(pairs > 0)
    def _():
        start_pair(0)

    def pair(j, carry):
        for copy in pair_copies(buf, saved_ref, sem, j, False):
            copy.wait()

        @pl.when(j + DEEP - 1 < pairs)
        def _():
            fetch(j + DEEP - 1, carry)

        act = buf.at[lax.rem(j, DEEP)]
        ray = jnp.concatenate([rays_ref[slots[2 * j]], rays_ref[slots[2 * j + 1]]], 1)
        dz3[CHID:, :] = d_logits[...]

        def through(grad, lo_row, hi_row, part):
            value = act[lo_row:hi_row, part].astype(jnp.float32)
            return grad * (1.0 - jnp.exp(-value))

        lanes = lane_parts(PARTS_B)
        d_feature = []
        for part in lanes:
            piece = through(mm(radt[...], dz3[CHID:, part]), R_S, R_END, part)
            dz3[:CHID, part] = piece.astype(jnp.bfloat16)
            d_feature.append(piece)
        d_ray = sum(over_samples(jnp.concatenate(d_feature, 1))).astype(jnp.bfloat16)
        start_pair(jnp.minimum(j + 1, pairs - 1))
        for wt, src, dst, lo, hi in (
            (fdt, dz3, dz2, R_H3, R_S), (t2, dz2, dz1, R_H2, R_H3), (t1, dz1, dz0, R_H1, R_H2)
        ):
            for part in lanes:
                dst[:, part] = through(mm(wt[...], src[:, part]), lo, hi, part).astype(jnp.bfloat16)
            if src is dz3:
                d_app = mm(code_ref[0], d_ray)
                hot, high = hot_lanes(ray[6:7].astype(jnp.int32))
                spread = jnp.concatenate(
                    [jnp.where(high == h, d_app, 0.0).astype(jnp.bfloat16) for h in range(SLOTS)], 0
                )
                g_ray[...] += mm_nt(d_ray, raycode_ref[j])
                g_rad[...] += mm_nt(act[R_S:R_END, :], dz3[CHID:, :])
                d_both = mm_nt(dz3[...], act[R_H3:R_S, :])
                g_ref[G_FEAT:G_TAB, :] += d_both[:CHID]
                g_ref[G_DEN : G_DEN + 16, 128:256] += d_both[CHID:, :128]
                g_ref[G_DEN + 16 : G_DEN + 32, 128:256] += d_both[CHID:, 128:]
                g_ref[G_TAB:G_POS, :] += mm_nt(spread, hot)
            elif src is dz2:
                g_ref[G_T2:G_FEAT, :] += mm_nt(dz2[...], act[R_H2:R_H3, :])
            else:
                g_ref[G_T1:G_T2, :] += mm_nt(dz1[...], act[R_H1:R_H2, :])
        g_pos[...] += mm_nt(dz0[...], act[:PC, :])
        return carry

    lax.fori_loop(0, pairs, pair, jnp.int32(0))

    def pick(a, select):
        return lax.dot_general(
            select.astype(jnp.float32), a, (((1,), (1,)), ((), ())),
            preferred_element_type=jnp.float32, precision=lax.Precision.HIGHEST,
        )

    g_ref[G_POS : G_POS + 63, :] = pick(g_pos[...], pos_select_ref[...])
    g_ref[G_VIEW : G_VIEW + 27, :128] = pick(g_ray[:, :VC], view_select_ref[...])
    g_ref[G_CODE : G_CODE + E, :128] = g_ray[...].T[VC:]
    g_ref[G_RAD:G_DEN, 128:256] = g_rad[...].T


def unpack_kernel(
    g_ref, got_colors_ref,
    colors_ref, pos_ref, trunk_ref, density_ref, feature_ref, view_ref, code_ref, radiance_ref, table_ref,
):
    colors_ref[...] = got_colors_ref[...]
    for n in range(63):
        pos_ref[n] = g_ref[G_POS + n : G_POS + n + 1, :]
    trunk_ref[0, 0] = g_ref[G_T1:G_T2, :]
    trunk_ref[0, 1] = g_ref[G_T2:G_FEAT, :]
    feature_ref[0] = g_ref[G_FEAT:G_TAB, :]
    density_ref[:, :128] = g_ref[G_DEN + 3 : G_DEN + 4, 128:256]
    density_ref[:, 128:] = g_ref[G_DEN + 19 : G_DEN + 20, 128:256]
    for n in range(27):
        view_ref[n] = g_ref[G_VIEW + n : G_VIEW + n + 1, :128]
    code_ref[0] = g_ref[G_CODE : G_CODE + E, :128]
    for n in range(3):
        radiance_ref[n] = g_ref[G_RAD + n : G_RAD + n + 1, 128:256]
    for h in range(SLOTS):
        table_ref[0, :, h * LO : (h + 1) * LO] = g_ref[G_TAB + h * E : G_TAB + (h + 1) * E, :]


VMEM = pl.BlockSpec(memory_space=pltpu.VMEM)
SMEM = pl.BlockSpec(memory_space=pltpu.SMEM)
ANY = pl.BlockSpec(memory_space=pl.ANY)
HBM = pl.BlockSpec(memory_space=pltpu.HBM)


def run_forward(live, center, rays, pos, trunk, density, feature, view, code, radiance, table):
    bf = jnp.bfloat16
    return pl.pallas_call(
        forward_kernel,
        name="forward_tiles",
        out_shape=(
            jax.ShapeDtypeStruct((SLOTS, 4, TILE), jnp.float32),
            jax.ShapeDtypeStruct((SLOTS // 2, R_END, 2 * LANES), bf),
            jax.ShapeDtypeStruct((SLOTS // 2, RC, 2 * TILE), bf),
            jax.ShapeDtypeStruct((SLOTS // 2, 8, 2 * LANES), jnp.float32),
        ),
        in_specs=[SMEM, SMEM] + [VMEM] * 11,
        out_specs=(VMEM, ANY, VMEM, VMEM),
        scratch_shapes=[
            pltpu.VMEM((HID, PC), bf),
            pltpu.VMEM((CHID + 16, HID), bf),
            pltpu.VMEM((CHID, RC), bf),
            pltpu.VMEM((8, CHID), bf),
            pltpu.VMEM((SLOTS * E, LO), bf),
            pltpu.VMEM((DEEP, R_END, 2 * LANES), bf),
            pltpu.SMEM((SLOTS + 1,), jnp.int32),
            pltpu.SemaphoreType.DMA((DEEP, 4)),
        ],
        compiler_params=pltpu.CompilerParams(vmem_limit_bytes=40 * 1024 * 1024),
        cost_estimate=pl.CostEstimate(flops=10**10, bytes_accessed=3 * 10**7, transcendentals=0),
    )(live, center, rays, pos, trunk, density, feature, view, code, radiance, table,
      jnp.asarray(POS_SELECT, bf), jnp.asarray(VIEW_SELECT, bf))


def run_backward(live, center, rays, cot, saved, raycode, small, trunk, density, feature, code, radiance):
    bf = jnp.bfloat16
    return pl.pallas_call(
        backward_kernel,
        name="backward_tiles",
        out_shape=jax.ShapeDtypeStruct((G_ROWS, 256), jnp.float32),
        in_specs=[SMEM, SMEM, VMEM, VMEM, ANY] + [VMEM] * 9,
        out_specs=VMEM,
        scratch_shapes=[
            pltpu.VMEM((HID, HID), bf),
            pltpu.VMEM((HID, HID), bf),
            pltpu.VMEM((HID, CHID + 16), bf),
            pltpu.VMEM((CHID, 16), bf),
            pltpu.VMEM((HID, 2 * LANES), bf),
            pltpu.VMEM((HID, 2 * LANES), bf),
            pltpu.VMEM((HID, 2 * LANES), bf),
            pltpu.VMEM((CHID + 16, 2 * LANES), bf),
            pltpu.VMEM((16, 2 * LANES), bf),
            pltpu.VMEM((HID, PC), jnp.float32),
            pltpu.VMEM((CHID, RC), jnp.float32),
            pltpu.VMEM((CHID, 16), jnp.float32),
            pltpu.VMEM((DEEP, R_END, 2 * LANES), bf),
            pltpu.SMEM((SLOTS + 1,), jnp.int32),
            pltpu.SemaphoreType.DMA((DEEP, 4)),
        ],
        compiler_params=pltpu.CompilerParams(vmem_limit_bytes=40 * 1024 * 1024),
        cost_estimate=pl.CostEstimate(flops=2 * 10**10, bytes_accessed=3 * 10**7, transcendentals=0),
    )(live, center, rays, cot, saved, raycode, small, trunk, density, feature, code, radiance,
      jnp.asarray(POS_SELECT, bf), jnp.asarray(VIEW_SELECT, bf))


def run_unpack(packed, colors):
    f32 = jnp.float32
    shapes = [colors.shape, (63, 1, 256), (1, 2, 256, 256), (1, 256), (1, 128, 256), (27, 1, 128),
              (1, 32, 128), (3, 1, 128), (1, 32, 8192)]
    outs = pl.pallas_call(
        unpack_kernel,
        name="unpack_gradients",
        out_shape=tuple(jax.ShapeDtypeStruct(s, f32) for s in shapes),
        in_specs=[VMEM] * 2,
        out_specs=tuple(VMEM for _ in shapes),
        compiler_params=pltpu.CompilerParams(vmem_limit_bytes=32 * 1024 * 1024),
    )(packed, colors)
    colors, pos, trunk, density, feature, view, code, radiance, table = outs
    return (
        colors, pos.transpose(1, 2, 0), trunk, density, feature, view.transpose(1, 2, 0),
        code.transpose(0, 2, 1), radiance.transpose(1, 0, 2), table,
    )


MESH = pl.DeviceIdType.MESH
GROUP = SLOTS
REPS = 4
CHUNK = G_ROWS // (4 * REPS)


def place():
    return lax.axis_index("blk"), lax.axis_index("rep")


def partner(blk, rep, i):
    return lax.rem(blk + i, GROUP), lax.rem(rep + GROUP * REPS - i, REPS)


def greet(blk, rep):
    barrier = pltpu.get_barrier_semaphore()
    for i in range(1, GROUP):
        pl.semaphore_signal(barrier, inc=1, device_id=partner(blk, rep, i), device_id_type=MESH)


def await_all():
    pl.semaphore_wait(pltpu.get_barrier_semaphore(), GROUP - 1)


def exchange(blk, rep, src, dst, send_sem, recv_sem):
    for i in range(1, GROUP):
        to_blk, to_rep = partner(blk, rep, i)
        pltpu.make_async_remote_copy(
            src_ref=src.at[to_blk], dst_ref=dst.at[blk], send_sem=send_sem,
            recv_sem=recv_sem, device_id=(to_blk, to_rep), device_id_type=MESH,
        ).start()
    dst[blk] = src[blk]
    most = pl.ds(0, GROUP - 1)
    return pltpu.make_async_remote_copy(
        src_ref=src.at[most], dst_ref=dst.at[most], send_sem=send_sem, recv_sem=recv_sem,
        device_id=partner(blk, rep, 1), device_id_type=MESH,
    )


def finish(everything):
    everything.wait_recv()
    everything.wait_send()


def find_tiles(ids_ref, tile_of, live):
    for k in range(GROUP):
        where, count = jnp.int32(0), jnp.int32(0)
        for t in range(ids_ref.shape[1]):
            for n in range(3):
                hit = ids_ref[n, t] == k
                where, count = jnp.where(hit, t, where), jnp.where(hit, 1, count)
        tile_of[k] = where
        if live is not None:
            live[k] = count


def scatter_kernel(
    ids_ref, anchors_ref, directions_ref, codes_ref, out_ref,
    tiles, send, anchors, directions, codes, tile_of, live, send_sem, recv_sem, sem,
):
    blk, rep = place()
    fetches = [
        pltpu.make_async_copy(src, dst, sem.at[n])
        for n, (src, dst) in enumerate(
            ((anchors_ref, anchors), (directions_ref, directions), (codes_ref, codes))
        )
    ]
    for fetch in fetches:
        fetch.start()
    greet(blk, rep)
    find_tiles(ids_ref, tile_of, live)
    for fetch in fetches:
        fetch.wait()
    row = row_iota(8, TILE)
    for t in range(tiles.shape[0]):
        lanes = slice(t * TILE, (t + 1) * TILE)
        tiles[t, 0:3] = anchors[:, lanes]
        tiles[t, 3:6] = directions[:, lanes]
        tiles[t, 6:7] = codes[t : t + 1, :].astype(jnp.float32)
        tiles[t, 7:8] = jnp.zeros((1, TILE), jnp.float32)
    for k in range(GROUP):
        send[k] = jnp.where(row == 7, live[k].astype(jnp.float32), tiles[tile_of[k]])
    await_all()
    finish(exchange(blk, rep, send, out_ref, send_sem, recv_sem))


def blend_kernel(
    ids_ref, part_ref, grad_ref, colors_ref, cot_ref,
    back, cots, send, tile_of, send_sem, recv_sem, send_sem2, recv_sem2,
):
    blk, rep = place()
    greet(blk, rep)
    await_all()
    partials = exchange(blk, rep, part_ref, back, send_sem, recv_sem)
    find_tiles(ids_ref, tile_of, None)
    finish(partials)
    for t in range(cots.shape[0]):
        summed = back[ids_ref[0, t]] + back[ids_ref[1, t]] + back[ids_ref[2, t]]
        lanes = slice(t * TILE, (t + 1) * TILE)
        colors = summed[:3] / summed[3:4]
        colors_ref[:, lanes] = colors
        cot = grad_ref[:, lanes] * LOSS_SCALE / summed[3:4]
        cots[t] = jnp.concatenate([cot, -jnp.sum(cot * colors, 0, keepdims=True)], 0)
    for k in range(GROUP):
        send[k] = cots[tile_of[k]]
    finish(exchange(blk, rep, send, cot_ref, send_sem2, recv_sem2))


def total_kernel(g_ref, out_ref, got, held, send_sem, recv_sem):
    blk, rep = place()
    up, down = lax.rem(rep + 1, REPS), lax.rem(rep + REPS - 1, REPS)
    barrier = pltpu.get_barrier_semaphore()
    for other in (up, down):
        pl.semaphore_signal(barrier, inc=1, device_id=(blk, other), device_id_type=MESH)
    pl.semaphore_wait(barrier, 2)
    rings = range(4)

    def chunk(ring, ahead):
        sign = 1 if ring % 2 == 0 else REPS - 1
        which = lax.rem(rep + sign * (ahead + REPS), REPS)
        return pl.ds(pl.multiple_of((ring * REPS + which) * CHUNK, 8), CHUNK)

    def copy(ring, step):
        if step == 0:
            src, dst = g_ref.at[chunk(ring, 0)], got.at[ring, 0]
        elif step < 3:
            src, dst = held.at[ring, step - 1], got.at[ring, step]
        else:
            rows = chunk(ring, 4 - step)
            src, dst = out_ref.at[rows], out_ref.at[rows]
        return pltpu.make_async_remote_copy(
            src_ref=src, dst_ref=dst, send_sem=send_sem.at[ring, step],
            recv_sem=recv_sem.at[ring, step],
            device_id=(blk, up if ring % 2 == 0 else down), device_id_type=MESH,
        )

    for ring in rings:
        copy(ring, 0).start()
    for step in range(6):
        for ring in rings:
            copy(ring, step).wait_recv()
            if step < 2:
                held[ring, step] = got[ring, step] + g_ref[chunk(ring, -step - 1), :]
            elif step == 2:
                out_ref[chunk(ring, 1), :] = got[ring, 2] + g_ref[chunk(ring, 1), :]
            if step < 5:
                copy(ring, step + 1).start()
    for step in range(6):
        for ring in rings:
            copy(ring, step).wait_send()


def communicate(kernel, name, number, args, specs, shapes, scratch):
    return pl.pallas_call(
        kernel,
        name=name,
        out_shape=shapes,
        in_specs=specs,
        out_specs=jax.tree.map(lambda _: VMEM, shapes),
        scratch_shapes=scratch,
        compiler_params=pltpu.CompilerParams(
            collective_id=number, has_side_effects=True, vmem_limit_bytes=16 * 1024 * 1024
        ),
        cost_estimate=pl.CostEstimate(flops=10**10, bytes_accessed=10**6, transcendentals=0),
    )(*args)


def run_scatter(ids, anchors, directions, codes):
    f32, i32 = jnp.float32, jnp.int32
    return communicate(
        scatter_kernel, "scatter_rays", 0, (ids, anchors, directions, codes), [SMEM, HBM, HBM, HBM],
        jax.ShapeDtypeStruct((GROUP, 8, TILE), f32),
        [pltpu.VMEM((codes.shape[0], 8, TILE), f32), pltpu.VMEM((GROUP, 8, TILE), f32),
         pltpu.VMEM(anchors.shape, f32), pltpu.VMEM(directions.shape, f32),
         pltpu.VMEM(codes.shape, i32), pltpu.SMEM((GROUP,), i32), pltpu.SMEM((GROUP,), i32)]
        + [pltpu.SemaphoreType.DMA] * 2 + [pltpu.SemaphoreType.DMA((3,))],
    )


def run_blend(ids, part, grad):
    tiles = grad.shape[1] // TILE
    small = (GROUP, 4, TILE)
    return communicate(
        blend_kernel, "blend_colors", 1, (ids, part, grad), [SMEM, VMEM, VMEM],
        (jax.ShapeDtypeStruct(grad.shape, jnp.float32), jax.ShapeDtypeStruct(small, jnp.float32)),
        [pltpu.VMEM(small, jnp.float32), pltpu.VMEM((tiles, 4, TILE), jnp.float32),
         pltpu.VMEM(small, jnp.float32), pltpu.SMEM((GROUP,), jnp.int32)]
        + [pltpu.SemaphoreType.DMA] * 4,
    )


def run_total(packed):
    return communicate(
        total_kernel, "total_gradients", 2, (packed,), [VMEM],
        jax.ShapeDtypeStruct((G_ROWS, 256), jnp.float32),
        [pltpu.VMEM((4, 3, CHUNK, 256), jnp.float32), pltpu.VMEM((4, 2, CHUNK, 256), jnp.float32)]
        + [pltpu.SemaphoreType.DMA((4, 6))] * 2,
    )


def local(
    anchors, directions, app_ids, block_ids, color_grad, block_centers, pos_weight, trunk_weight,
    density_weight, feature_weight, view_weight, code_weight, radiance_weight, code_table,
):
    tiles = block_ids.shape[0]
    ids = block_ids.T
    rays = run_scatter(ids, anchors, directions, app_ids.reshape(tiles, TILE))
    live = (rays[:, 7, 0] > 0.5).astype(jnp.int32)
    center = block_centers.T
    code = code_weight.transpose(0, 2, 1)
    part, saved, raycode, small = run_forward(
        live, center, rays, pos_weight.transpose(0, 2, 1), trunk_weight, density_weight, feature_weight,
        view_weight.transpose(0, 2, 1), code, radiance_weight, code_table,
    )
    colors, cot = run_blend(ids, part, color_grad)
    packed = run_backward(
        live, center, rays, cot, saved, raycode, small, trunk_weight, density_weight,
        feature_weight, code, radiance_weight,
    )
    return run_unpack(run_total(packed), colors)


def solution(mesh):
    weights = (P("blk", None, None), P("blk", None, None, None), P("blk", None)) + (
        P("blk", None, None),
    ) * 5
    ray = P(None, ("blk", "rep"))
    return jax.shard_map(
        local,
        mesh=mesh,
        in_specs=(ray, ray, P(("blk", "rep")), P(("blk", "rep"), None), ray, P(None, "blk")) + weights,
        out_specs=(ray,) + weights,
        check_vma=False,
    )
```

profile of v0, /device:TPU:1, one launch (start us, length us, event | category | flops | bytes accessed | tf_op | source)
XLA Modules:
  0.0 108.8 jit_solution(5419728818791349540)
XLA Ops:
  0.6 0.0 copy-start.4
  0.7 0.7 copy-done.4
  1.4 0.0 copy-start.5
  1.4 0.7 copy-done.5
  2.1 0.0 copy-start.9
  2.1 0.7 copy-done.9
  2.7 0.0 copy-start.10
  2.7 0.7 copy-done.10
  3.4 0.0 copy-start
  3.4 0.0 copy-start.1
  3.4 0.0 copy-start.2
  3.4 0.0 copy-start.3
  3.4 0.0 copy-start.7
  3.4 0.0 copy-start.8
  3.5 0.0 copy-start.12
  3.5 0.0 copy-start.13
  3.5 0.0 copy-start.14
  3.5 0.0 copy-start.15
  3.5 0.0 copy-start.16
  3.5 15.2 %scatter_rays.1.rays_ref = f32[32,8,128]{2,1,0:T(8,128)S(1)} custom-call(s32[3,5]{1,0:T(4,128)S(1)} %bitcast.15, f32[3,640]{1,0:T(4,128)S(1)} %copy-done.4, f32[3,640]{1,0:T(4,128)S(1)} %copy-done.5, s32[5,128]{1,0:T(8,128)S(1)} %bitcast.14), custom_call_target="tpu_custom_call" | custom-call | flops 10000000000 | bytes 1000000 | tf_op jit(solution)/shard_map/scatter_rays/pallas_call | solution.py:683
  18.7 0.7 fusion.live_ref
  19.4 0.0 copy-done
  19.4 0.0 copy-done.1
  19.4 0.0 copy-done.2
  19.4 0.0 copy-done.3
  19.4 0.0 copy-done.7
  19.4 0.0 copy-done.8
  19.4 0.0 copy-done.12
  19.4 0.0 copy-done.13
  19.5 0.0 copy-done.14
  19.5 0.0 copy-done.15
  19.5 0.0 copy-done.16
  19.5 0.0 copy-start.6
  19.5 0.0 copy-start.11
  19.5 20.4 %forward_tiles.1 = (f32[32,4,128]{2,1,0:T(4,128)S(1)}, bf16[16,992,1024]{2,1,0:T(8,128)(2,1)}, bf16[16,80,256]{2,1,0:T(8,128)(2,1)S(1)}, f32[16,8,1024]{2,1,0:T(8,128)S(1)}) custom-call(s32[32]{0:T(128)S(1)} %fusion.live_ref, f32[1,3]{1,0:T(1,128)S(1)} %bitcast.17, f32[32,8,128]{2,1,0:T(8,128)S(1)} %scatter_rays.1.rays_ref, ...), custom_call_target="tpu_custom_call" | custom-call | flops 10000000000 | bytes 30000000 | tf_op jit(solution)/shard_map/forward_tiles/pallas_call | solution.py:453
  39.9 0.0 copy-done.6
  39.9 0.0 copy-done.11
  39.9 15.0 %blend_colors.1 = (f32[3,640]{1,0:T(4,128)S(1)}, f32[32,4,128]{2,1,0:T(4,128)S(1)}) custom-call(s32[3,5]{1,0:T(4,128)S(1)} %bitcast.16, f32[32,4,128]{2,1,0:T(4,128)S(1)} %get-tuple-element.24.part_ref, f32[3,640]{1,0:T(4,128)S(1)} %copy-done.6), custom_call_target="tpu_custom_call" | custom-call | flops 10000000000 | bytes 1000000 | tf_op jit(solution)/shard_map/blend_colors/pallas_call | solution.py:683
  55.0 20.4 %backward_tiles.1.g_ref = f32[1792,256]{1,0:T(8,128)S(1)} custom-call(s32[32]{0:T(128)S(1)} %fusion.live_ref, f32[1,3]{1,0:T(1,128)S(1)} %bitcast.18, f32[32,8,128]{2,1,0:T(8,128)S(1)} %scatter_rays.1.rays_ref, f32[32,4,128]{2,1,0:T(4,128)S(1)} %get-tuple-element.25.cot_ref, bf16[16,992,1024]{2,1,0:T(8,128)(2,1)} %get-tuple-element.26.saved_ref, ...), custom_call_target="tpu_custom_call" | custom-call | flops 20000000000 | bytes 30000000 | tf_op jit(solution)/shard_map/backward_tiles/pallas_call | solution.py:482
  75.4 32.0 %total_gradients.1.g_ref = f32[1792,256]{1,0:T(8,128)S(1)} custom-call(f32[1792,256]{1,0:T(8,128)S(1)} %backward_tiles.1.g_ref), custom_call_target="tpu_custom_call" | custom-call | flops 10000000000 | bytes 1000000 | tf_op jit(solution)/shard_map/total_gradients/pallas_call | solution.py:683
  107.4 1.4 %unpack_gradients.1 = (f32[3,640]{1,0:T(4,128)}, f32[63,1,256]{2,1,0:T(1,128)}, f32[1,2,256,256]{3,2,1,0:T(8,128)}, f32[1,256]{1,0:T(1,128)}, f32[1,128,256]{2,1...) custom-call(f32[1792,256]{1,0:T(8,128)S(1)} %total_gradients.1.g_ref, ...), custom_call_target="tpu_custom_call" | custom-call | tf_op jit(solution)/shard_map/unpack_gradients/pallas_call | solution.py:515
Async XLA Ops:
  0.6 0.7 copy-start.4
  1.4 0.7 copy-start.5
  2.1 0.7 copy-start.9
  2.7 0.7 copy-start.10
  3.4 16.0 %copy-start = (bf16[1,32,8192]{2,1,0:T(8,128)(2,1)S(1)}, bf16[1,32,8192]{2,1,0:T(8,128)(2,1)}, u32[]{:S(2)}) copy-start(bf16[1,32,8192]{2,1,0:T(8,128)(2,1)} %table_ref.1) | copy-start | bytes 1572868
  3.4 16.0 %copy-start.1 = (bf16[1,2,256,256]{3,2,1,0:T(8,128)(2,1)S(1)}, bf16[1,2,256,256]{3,2,1,0:T(8,128)(2,1)}, u32[]{:S(2)}) copy-start(bf16[1,2,256,256]{3,2,1,0:T(8,128)(2,1)} %trunk_ref.3) | copy-start | bytes 786436
  3.4 16.0 %copy-start.2 = (bf16[1,128,256]{2,1,0:T(8,128)(2,1)S(1)}, bf16[1,128,256]{2,1,0:T(8,128)(2,1)}, u32[]{:S(2)}) copy-start(bf16[1,128,256]{2,1,0:T(8,128)(2,1)} %feature_ref.3) | copy-start | bytes 196612
  3.4 16.0 %copy-start.3 = (bf16[1,256,63]{1,2,0:T(8,128)(2,1)S(1)}, bf16[1,256,63]{1,2,0:T(8,128)(2,1)}, u32[]{:S(2)}) copy-start(bf16[1,256,63]{1,2,0:T(8,128)(2,1)} %param.24) | copy-start | bytes 96772
  3.4 16.0 %copy-start.7 = (bf16[1,128,27]{1,2,0:T(8,128)(2,1)S(1)}, bf16[1,128,27]{1,2,0:T(8,128)(2,1)}, u32[]{:S(2)}) copy-start(bf16[1,128,27]{1,2,0:T(8,128)(2,1)} %param.28) | copy-start | bytes 20740
  3.4 16.0 %copy-start.8 = (bf16[1,128,32]{1,2,0:T(8,128)(2,1)S(1)}, bf16[1,128,32]{1,2,0:T(8,128)(2,1)}, u32[]{:S(2)}) copy-start(bf16[1,128,32]{1,2,0:T(8,128)(2,1)} %param.29) | copy-start | bytes 24580
  3.5 16.0 %copy-start.12 = (bf16[1,256]{1,0:T(2,128)(2,1)S(1)}, bf16[1,256]{1,0:T(2,128)(2,1)}, u32[]{:S(2)}) copy-start(bf16[1,256]{1,0:T(2,128)(2,1)} %density_ref.3) | copy-start | bytes 1540
  3.5 16.0 %copy-start.13 = (bf16[1,3,128]{2,1,0:T(4,128)(2,1)S(1)}, bf16[1,3,128]{2,1,0:T(4,128)(2,1)}, u32[]{:S(2)}) copy-start(bf16[1,3,128]{2,1,0:T(4,128)(2,1)} %radiance_ref.3) | copy-start | bytes 2308
  3.5 16.0 %copy-start.14 = (f32[3,1]{0,1:T(1,128)S(1)}, f32[3,1]{0,1:T(1,128)}, u32[]{:S(2)}) copy-start(f32[3,1]{0,1:T(1,128)} %param.23) | copy-start | bytes 40
  3.5 16.0 %copy-start.15 = (bf16[63,96]{1,0:T(8,128)(2,1)S(1)}, bf16[63,96]{1,0:T(8,128)(2,1)}, u32[]{:S(2)}) copy-start(bf16[63,96]{1,0:T(8,128)(2,1)} %constant.6.clone.pos_select_ref) | copy-start | bytes 36292
  3.5 16.0 %copy-start.16 = (bf16[27,48]{1,0:T(8,128)(2,1)S(1)}, bf16[27,48]{1,0:T(8,128)(2,1)}, u32[]{:S(2)}) copy-start(bf16[27,48]{1,0:T(8,128)(2,1)} %constant.7.clone.view_select_ref) | copy-start | bytes 7780
  19.5 20.4 %copy-start.6 = (f32[3,640]{1,0:T(4,128)S(1)}, f32[3,640]{1,0:T(4,128)}, u32[]{:S(2)}) copy-start(f32[3,640]{1,0:T(4,128)} %grad_ref.1) | copy-start | bytes 23044
  19.5 20.4 %copy-start.11 = (s32[5,3]{0,1:T(4,128)S(1)}, s32[5,3]{0,1:T(4,128)}, u32[]{:S(2)}) copy-start(s32[5,3]{0,1:T(4,128)} %param.21) | copy-start | bytes 184
where the time goes:
time: 109 us
  Pallas kernels  104 us (95%)
  local copies, waits for them, and re-layouts  2.83 us (3%)
    pallas_call x3, Pallas kernels, communicate(): pl.pallas_call(kernel, name=name, out_shape=shapes, in_specs=specs, out_s...  62.2 us
    pallas_call x1, Pallas kernels, run_forward(): pl.pallas_call(forward_kernel, name='forward_tiles', out_shape=(jax.Shape...  20.4 us
    pallas_call x1, Pallas kernels, run_backward(): pl.pallas_call(backward_kernel, name='backward_tiles', out_shape=jax.Shap...  20.4 us
    unnamed x34, local copies, waits for them, and re-layouts  2.83 us

commit v1 on v0

--- a/solution.py
+++ b/solution.py
@@ -31,16 +31,21 @@
 R_END = R_S + CHID
 GATHER_AFTER = R_H2
 
-G_T1 = 0
-G_T2 = 256
-G_FEAT = 512
-G_TAB = 640
-G_POS = 1664
-G_VIEW = 1728
-G_CODE = 1760
-G_RAD = 1728
-G_DEN = 1744
-G_ROWS = 1792
+G_TAB = 0
+G_FEAT = 1024
+G_VIEW = 1152
+G_CODE = 1184
+G_RAD = 1152
+G_DEN = 1168
+A_ROWS = 1280
+G_T1 = 1280
+G_T2 = 1536
+G_POS = 1792
+G_ROWS = 1920
+PAIRS = SLOTS // 2
+LOW = ((0, 208), (208, 416), (416, R_H3))
+HIGH = ((R_H3, 736), (736, R_S), (R_S, R_END))
+ALL = LOW + HIGH
 
 
 def code_places(levels, half):
@@ -179,11 +184,12 @@
     return total, (total + 1) // 2
 
 
-def pair_copies(buf, saved_ref, sem, j, out):
+def pair_copies(buf, saved_ref, sem, j, out, ranges):
     slot = lax.rem(j, DEEP)
+    base = ranges[0][0]
     copies = []
-    for n, (lo, hi) in enumerate(((0, 256), (256, 512), (512, 752), (752, R_END))):
-        near, far = buf.at[slot, lo:hi], saved_ref.at[j, lo:hi]
+    for n, (lo, hi) in enumerate(ranges):
+        near, far = buf.at[slot, lo - base : hi - base], saved_ref.at[j, lo:hi]
         src, dst = (near, far) if out else (far, near)
         copies.append(pltpu.make_async_copy(src, dst, sem.at[slot, n]))
     return copies
@@ -203,7 +209,7 @@
     live_ref, center_ref, rays_ref, pos_ref, trunk_ref, density_ref, feature_ref, view_ref,
     code_ref, radiance_ref, table_ref, pos_select_ref, view_select_ref,
     part_ref, saved_ref, raycode_ref, small_ref,
-    wp, wfd, wray, wrad, tab, buf, slots, sem,
+    wp, wfd, wray, wrad, tab, buf, slots, sem, blank_sem,
 ):
     row = row_iota(8, 2 * TILE)
     c8 = center_rows(center_ref, row)
@@ -234,7 +240,7 @@
     def pair(j, carry):
         @pl.when(j >= DEEP)
         def _():
-            for copy in pair_copies(buf, saved_ref, sem, j - DEEP, True):
+            for copy in pair_copies(buf, saved_ref, sem, j - DEEP, True, ALL):
                 copy.wait()
 
         out = buf.at[lax.rem(j, DEEP)]
@@ -273,7 +279,7 @@
             small.append(jnp.where(row_iota(8, logits.shape[1]) == 3, both[CHID : CHID + 8], logits))
         small = jnp.concatenate(small, 1)
         small_ref[j] = small
-        for copy in pair_copies(buf, saved_ref, sem, j, True):
+        for copy in pair_copies(buf, saved_ref, sem, j, True, ALL):
             copy.start()
         return carry
 
@@ -285,23 +291,49 @@
         finish_pair(pairs - 1)
 
     def drain(j, carry):
-        for copy in pair_copies(buf, saved_ref, sem, j, True):
+        for copy in pair_copies(buf, saved_ref, sem, j, True, ALL):
             copy.wait()
         return carry
 
     lax.fori_loop(jnp.maximum(pairs - DEEP, 0), pairs, drain, jnp.int32(0))
+    buf[0, :R_H3, :] = jnp.zeros((R_H3, 2 * LANES), jnp.bfloat16)
+
+    def blank(j):
+        return pltpu.make_async_copy(buf.at[0, :R_H3], saved_ref.at[j, :R_H3], blank_sem.at[j])
+
+    def begin_blank(j, carry):
+        blank(j).start()
+        return carry
+
+    def end_blank(j, carry):
+        blank(j).wait()
+        return carry
+
+    lax.fori_loop(pairs, PAIRS, begin_blank, jnp.int32(0))
+    lax.fori_loop(pairs, PAIRS, end_blank, jnp.int32(0))
+
+
+def flip(x):
+    return x.astype(jnp.float32).T.astype(jnp.bfloat16)
+
+
+def pick(a, select):
+    return lax.dot_general(
+        select.astype(jnp.float32), a, (((1,), (1,)), ((), ())),
+        preferred_element_type=jnp.float32, precision=lax.Precision.HIGHEST,
+    )
 
 
 def backward_kernel(
-    live_ref, center_ref, rays_ref, cot_ref, saved_ref, raycode_ref, small_ref, trunk_ref,
-    density_ref, feature_ref, code_ref, radiance_ref, pos_select_ref, view_select_ref,
-    g_ref,
-    t1, t2, fdt, radt, dz0, dz1, dz2, dz3, d_logits, g_pos, g_ray, g_rad, buf, slots, sem,
+    live_ref, center_ref, rays_ref, cot_ref, saved_ref, raycode_ref, small_ref,
+    density_ref, feature_ref, code_ref, radiance_ref, view_select_ref,
+    g_ref, dz_ref,
+    fdt, radt, dz3, d_logits, g_ray, g_rad, buf, slots, sem,
 ):
     total, pairs = list_live(live_ref, slots)
 
     def fetch(j, carry):
-        for copy in pair_copies(buf, saved_ref, sem, j, False):
+        for copy in pair_copies(buf, saved_ref, sem, j, False, HIGH):
             copy.start()
         return carry
 
@@ -310,11 +342,6 @@
     lane = lax.broadcasted_iota(jnp.int32, (1, 2 * TILE), 1)
     c8 = center_rows(center_ref, row)
 
-    def flip(x):
-        return x.astype(jnp.float32).T.astype(jnp.bfloat16)
-
-    t1[...] = flip(trunk_ref[0, 0])
-    t2[...] = flip(trunk_ref[0, 1])
     fdt[:, :CHID] = flip(feature_ref[0])
     row16 = row_iota(16, HID)
     fdt[:, CHID:] = jnp.where(row16 == 3, density_ref[...].astype(jnp.float32), 0.0).T.astype(jnp.bfloat16)
@@ -322,7 +349,12 @@
         [radiance_ref[0].astype(jnp.float32), jnp.zeros((13, CHID), jnp.float32)], 0
     ).T.astype(jnp.bfloat16)
     g_ref[...] = jnp.zeros_like(g_ref)
-    g_pos[...] = jnp.zeros_like(g_pos)
+
+    def blank(j, carry):
+        dz_ref[j] = jnp.zeros((HID, 2 * LANES), jnp.bfloat16)
+        return carry
+
+    lax.fori_loop(pairs, PAIRS, blank, jnp.int32(0))
     g_ray[...] = jnp.zeros_like(g_ray)
     g_rad[...] = jnp.zeros_like(g_rad)
 
@@ -359,7 +391,7 @@
         start_pair(0)
 
     def pair(j, carry):
-        for copy in pair_copies(buf, saved_ref, sem, j, False):
+        for copy in pair_copies(buf, saved_ref, sem, j, False, HIGH):
             copy.wait()
 
         @pl.when(j + DEEP - 1 < pairs)
@@ -371,7 +403,7 @@
         dz3[CHID:, :] = d_logits[...]
 
         def through(grad, lo_row, hi_row, part):
-            value = act[lo_row:hi_row, part].astype(jnp.float32)
+            value = act[lo_row - R_H3 : hi_row - R_H3, part].astype(jnp.float32)
             return grad * (1.0 - jnp.exp(-value))
 
         lanes = lane_parts(PARTS_B)
@@ -382,40 +414,23 @@
             d_feature.append(piece)
         d_ray = sum(over_samples(jnp.concatenate(d_feature, 1))).astype(jnp.bfloat16)
         start_pair(jnp.minimum(j + 1, pairs - 1))
-        for wt, src, dst, lo, hi in (
-            (fdt, dz3, dz2, R_H3, R_S), (t2, dz2, dz1, R_H2, R_H3), (t1, dz1, dz0, R_H1, R_H2)
-        ):
-            for part in lanes:
-                dst[:, part] = through(mm(wt[...], src[:, part]), lo, hi, part).astype(jnp.bfloat16)
-            if src is dz3:
-                d_app = mm(code_ref[0], d_ray)
-                hot, high = hot_lanes(ray[6:7].astype(jnp.int32))
-                spread = jnp.concatenate(
-                    [jnp.where(high == h, d_app, 0.0).astype(jnp.bfloat16) for h in range(SLOTS)], 0
-                )
-                g_ray[...] += mm_nt(d_ray, raycode_ref[j])
-                g_rad[...] += mm_nt(act[R_S:R_END, :], dz3[CHID:, :])
-                d_both = mm_nt(dz3[...], act[R_H3:R_S, :])
-                g_ref[G_FEAT:G_TAB, :] += d_both[:CHID]
-                g_ref[G_DEN : G_DEN + 16, 128:256] += d_both[CHID:, :128]
-                g_ref[G_DEN + 16 : G_DEN + 32, 128:256] += d_both[CHID:, 128:]
-                g_ref[G_TAB:G_POS, :] += mm_nt(spread, hot)
-            elif src is dz2:
-                g_ref[G_T2:G_FEAT, :] += mm_nt(dz2[...], act[R_H2:R_H3, :])
-            else:
-                g_ref[G_T1:G_T2, :] += mm_nt(dz1[...], act[R_H1:R_H2, :])
-        g_pos[...] += mm_nt(dz0[...], act[:PC, :])
+        for part in lanes:
+            dz_ref[j, :, part] = through(mm(fdt[...], dz3[:, part]), R_H3, R_S, part).astype(jnp.bfloat16)
+        d_app = mm(code_ref[0], d_ray)
+        hot, high = hot_lanes(ray[6:7].astype(jnp.int32))
+        spread = jnp.concatenate(
+            [jnp.where(high == h, d_app, 0.0).astype(jnp.bfloat16) for h in range(SLOTS)], 0
+        )
+        g_ray[...] += mm_nt(d_ray, raycode_ref[j])
+        g_rad[...] += mm_nt(act[HID:, :], dz3[CHID:, :])
+        d_both = mm_nt(dz3[...], act[:HID, :])
+        g_ref[G_FEAT:G_VIEW, :] += d_both[:CHID]
+        g_ref[G_DEN : G_DEN + 16, 128:256] += d_both[CHID:, :128]
+        g_ref[G_DEN + 16 : G_DEN + 32, 128:256] += d_both[CHID:, 128:]
+        g_ref[G_TAB:G_FEAT, :] += mm_nt(spread, hot)
         return carry
 
     lax.fori_loop(0, pairs, pair, jnp.int32(0))
-
-    def pick(a, select):
-        return lax.dot_general(
-            select.astype(jnp.float32), a, (((1,), (1,)), ((), ())),
-            preferred_element_type=jnp.float32, precision=lax.Precision.HIGHEST,
-        )
-
-    g_ref[G_POS : G_POS + 63, :] = pick(g_pos[...], pos_select_ref[...])
     g_ref[G_VIEW : G_VIEW + 27, :128] = pick(g_ray[:, :VC], view_select_ref[...])
     g_ref[G_CODE : G_CODE + E, :128] = g_ray[...].T[VC:]
     g_ref[G_RAD:G_DEN, 128:256] = g_rad[...].T
@@ -429,8 +444,8 @@
     for n in range(63):
         pos_ref[n] = g_ref[G_POS + n : G_POS + n + 1, :]
     trunk_ref[0, 0] = g_ref[G_T1:G_T2, :]
-    trunk_ref[0, 1] = g_ref[G_T2:G_FEAT, :]
-    feature_ref[0] = g_ref[G_FEAT:G_TAB, :]
+    trunk_ref[0, 1] = g_ref[G_T2:G_POS, :]
+    feature_ref[0] = g_ref[G_FEAT:G_VIEW, :]
     density_ref[:, :128] = g_ref[G_DEN + 3 : G_DEN + 4, 128:256]
     density_ref[:, 128:] = g_ref[G_DEN + 19 : G_DEN + 20, 128:256]
     for n in range(27):
@@ -469,43 +484,41 @@
             pltpu.VMEM((SLOTS * E, LO), bf),
             pltpu.VMEM((DEEP, R_END, 2 * LANES), bf),
             pltpu.SMEM((SLOTS + 1,), jnp.int32),
-            pltpu.SemaphoreType.DMA((DEEP, 4)),
+            pltpu.SemaphoreType.DMA((DEEP, len(ALL))),
+            pltpu.SemaphoreType.DMA((PAIRS,)),
         ],
-        compiler_params=pltpu.CompilerParams(vmem_limit_bytes=40 * 1024 * 1024),
+        compiler_params=pltpu.CompilerParams(vmem_limit_bytes=32 * 1024 * 1024),
         cost_estimate=pl.CostEstimate(flops=10**10, bytes_accessed=3 * 10**7, transcendentals=0),
     )(live, center, rays, pos, trunk, density, feature, view, code, radiance, table,
       jnp.asarray(POS_SELECT, bf), jnp.asarray(VIEW_SELECT, bf))
 
 
-def run_backward(live, center, rays, cot, saved, raycode, small, trunk, density, feature, code, radiance):
+def run_backward(live, center, rays, cot, saved, raycode, small, density, feature, code, radiance):
     bf = jnp.bfloat16
     return pl.pallas_call(
         backward_kernel,
         name="backward_tiles",
-        out_shape=jax.ShapeDtypeStruct((G_ROWS, 256), jnp.float32),
-        in_specs=[SMEM, SMEM, VMEM, VMEM, ANY] + [VMEM] * 9,
-        out_specs=VMEM,
+        out_shape=(
+            jax.ShapeDtypeStruct((A_ROWS, 256), jnp.float32),
+            jax.ShapeDtypeStruct((PAIRS, HID, 2 * LANES), bf),
+        ),
+        in_specs=[SMEM, SMEM, VMEM, VMEM, ANY] + [VMEM] * 7,
+        out_specs=(VMEM, VMEM),
         scratch_shapes=[
-            pltpu.VMEM((HID, HID), bf),
-            pltpu.VMEM((HID, HID), bf),
             pltpu.VMEM((HID, CHID + 16), bf),
             pltpu.VMEM((CHID, 16), bf),
-            pltpu.VMEM((HID, 2 * LANES), bf),
-            pltpu.VMEM((HID, 2 * LANES), bf),
-            pltpu.VMEM((HID, 2 * LANES), bf),
             pltpu.VMEM((CHID + 16, 2 * LANES), bf),
             pltpu.VMEM((16, 2 * LANES), bf),
-            pltpu.VMEM((HID, PC), jnp.float32),
             pltpu.VMEM((CHID, RC), jnp.float32),
             pltpu.VMEM((CHID, 16), jnp.float32),
-            pltpu.VMEM((DEEP, R_END, 2 * LANES), bf),
+            pltpu.VMEM((DEEP, R_END - R_H3, 2 * LANES), bf),
             pltpu.SMEM((SLOTS + 1,), jnp.int32),
-            pltpu.SemaphoreType.DMA((DEEP, 4)),
+            pltpu.SemaphoreType.DMA((DEEP, len(HIGH))),
         ],
-        compiler_params=pltpu.CompilerParams(vmem_limit_bytes=40 * 1024 * 1024),
-        cost_estimate=pl.CostEstimate(flops=2 * 10**10, bytes_accessed=3 * 10**7, transcendentals=0),
-    )(live, center, rays, cot, saved, raycode, small, trunk, density, feature, code, radiance,
-      jnp.asarray(POS_SELECT, bf), jnp.asarray(VIEW_SELECT, bf))
+        compiler_params=pltpu.CompilerParams(vmem_limit_bytes=32 * 1024 * 1024),
+        cost_estimate=pl.CostEstimate(flops=10**10, bytes_accessed=10**7, transcendentals=0),
+    )(live, center, rays, cot, saved, raycode, small, density, feature, code, radiance,
+      jnp.asarray(VIEW_SELECT, bf))
 
 
 def run_unpack(packed, colors):
@@ -530,7 +543,6 @@
 MESH = pl.DeviceIdType.MESH
 GROUP = SLOTS
 REPS = 4
-CHUNK = G_ROWS // (4 * REPS)
 
 
 def place():
@@ -635,48 +647,115 @@
     finish(exchange(blk, rep, send, cot_ref, send_sem2, recv_sem2))
 
 
-def total_kernel(g_ref, out_ref, got, held, send_sem, recv_sem):
+class Rings:
+    def __init__(self, blk, rep, g, out, base, got, held, send_sem, recv_sem):
+        self.blk, self.rep, self.g, self.out, self.base = blk, rep, g, out, base
+        self.got, self.held, self.send_sem, self.recv_sem = got, held, send_sem, recv_sem
+        self.rows = g.shape[0] // (4 * REPS)
+
+    def chunk(self, ring, ahead, base):
+        sign = 1 + (REPS - 2) * lax.rem(ring, 2)
+        which = lax.rem(self.rep + sign * (ahead + REPS), REPS)
+        return pl.ds(pl.multiple_of(base + (ring * REPS + which) * self.rows, 8), self.rows)
+
+    def copy(self, ring, step):
+        if step == 0:
+            src, dst = self.g.at[self.chunk(ring, 0, 0)], self.got.at[ring, 0]
+        elif step < 3:
+            src, dst = self.held.at[ring, step - 1], self.got.at[ring, step]
+        else:
+            rows = self.chunk(ring, 4 - step, self.base)
+            src, dst = self.out.at[rows], self.out.at[rows]
+        to = lax.rem(self.rep + 1 + (REPS - 2) * lax.rem(ring, 2), REPS)
+        return pltpu.make_async_remote_copy(
+            src_ref=src, dst_ref=dst, send_sem=self.send_sem.at[ring, step],
+            recv_sem=self.recv_sem.at[ring, step], device_id=(self.blk, to), device_id_type=MESH,
+        )
+
+    def each(self, action):
+        def body(ring, carry):
+            action(ring)
+            return carry
+
+        lax.fori_loop(0, 4, body, 0)
+
+    def begin(self):
+        self.each(lambda ring: self.copy(ring, 0).start())
+
+    def advance(self, ring, step):
+        self.copy(ring, step).wait_recv()
+        if step < 2:
+            mine = self.g[self.chunk(ring, -step - 1, 0), :]
+            self.held[ring, step] = self.got[ring, step] + mine
+        elif step == 2:
+            mine = self.g[self.chunk(ring, 1, 0), :]
+            self.out[self.chunk(ring, 1, self.base), :] = self.got[ring, 2] + mine
+        if step < 5:
+            self.copy(ring, step + 1).start()
+
+    def drain(self):
+        for step in range(6):
+            self.each(lambda ring: self.copy(ring, step).wait_send())
+
+
+def trunk_kernel(
+    ga_ref, dz_ref, trunk_ref, pos_select_ref, saved_ref, out_ref,
+    t1, t2, dz0, dz1, gb, g_pos, buf, sem, got_a, held_a, got_b, held_b, send_a, recv_a, send_b, recv_b,
+):
     blk, rep = place()
-    up, down = lax.rem(rep + 1, REPS), lax.rem(rep + REPS - 1, REPS)
     barrier = pltpu.get_barrier_semaphore()
-    for other in (up, down):
+    for other in (lax.rem(rep + 1, REPS), lax.rem(rep + REPS - 1, REPS)):
         pl.semaphore_signal(barrier, inc=1, device_id=(blk, other), device_id_type=MESH)
+    for first in range(DEEP - 1):
+        for copy in pair_copies(buf, saved_ref, sem, jnp.int32(first), False, LOW):
+            copy.start()
+    t1[...] = flip(trunk_ref[0, 0])
+    t2[...] = flip(trunk_ref[0, 1])
+    gb[...] = jnp.zeros_like(gb)
+    g_pos[...] = jnp.zeros_like(g_pos)
     pl.semaphore_wait(barrier, 2)
-    rings = range(4)
-
-    def chunk(ring, ahead):
-        sign = 1 if ring % 2 == 0 else REPS - 1
-        which = lax.rem(rep + sign * (ahead + REPS), REPS)
-        return pl.ds(pl.multiple_of((ring * REPS + which) * CHUNK, 8), CHUNK)
-
-    def copy(ring, step):
-        if step == 0:
-            src, dst = g_ref.at[chunk(ring, 0)], got.at[ring, 0]
-        elif step < 3:
-            src, dst = held.at[ring, step - 1], got.at[ring, step]
-        else:
-            rows = chunk(ring, 4 - step)
-            src, dst = out_ref.at[rows], out_ref.at[rows]
-        return pltpu.make_async_remote_copy(
-            src_ref=src, dst_ref=dst, send_sem=send_sem.at[ring, step],
-            recv_sem=recv_sem.at[ring, step],
-            device_id=(blk, up if ring % 2 == 0 else down), device_id_type=MESH,
-        )
-
-    for ring in rings:
-        copy(ring, 0).start()
+    color = Rings(blk, rep, ga_ref, out_ref, 0, got_a, held_a, send_a, recv_a)
+    trunk = Rings(blk, rep, gb, out_ref, A_ROWS, got_b, held_b, send_b, recv_b)
+    color.begin()
+    lanes = lane_parts(PARTS_B)
+
+    def pair(j):
+        for copy in pair_copies(buf, saved_ref, sem, j, False, LOW):
+            copy.wait()
+
+        @pl.when(j + DEEP - 1 < PAIRS)
+        def _():
+            for copy in pair_copies(buf, saved_ref, sem, j + DEEP - 1, False, LOW):
+                copy.start()
+
+        act = buf.at[lax.rem(j, DEEP)]
+        dz2 = dz_ref.at[j]
+        for wt, src, dst, lo, hi in ((t2, dz2, dz1, R_H2, R_H3), (t1, dz1, dz0, R_H1, R_H2)):
+            for part in lanes:
+                value = act[lo:hi, part].astype(jnp.float32)
+                grad = mm(wt[...], src[:, part]) * (1.0 - jnp.exp(-value))
+                dst[:, part] = grad.astype(jnp.bfloat16)
+            if src is dz2:
+                gb[HID : 2 * HID, :] += mm_nt(dz2[...], act[R_H2:R_H3, :])
+        gb[:HID, :] += mm_nt(dz1[...], act[R_H1:R_H2, :])
+        g_pos[...] += mm_nt(dz0[...], act[:PC, :])
+
+    for step in range(4):
+
+        def both(ring, carry):
+            pair(4 * step + ring)
+            color.advance(ring, step)
+            return carry
+
+        lax.fori_loop(0, 4, both, 0)
+    gb[2 * HID : 2 * HID + 63, :] = pick(g_pos[...], pos_select_ref[...])
+    trunk.begin()
+    for step in (4, 5):
+        color.each(lambda ring: color.advance(ring, step))
     for step in range(6):
-        for ring in rings:
-            copy(ring, step).wait_recv()
-            if step < 2:
-                held[ring, step] = got[ring, step] + g_ref[chunk(ring, -step - 1), :]
-            elif step == 2:
-                out_ref[chunk(ring, 1), :] = got[ring, 2] + g_ref[chunk(ring, 1), :]
-            if step < 5:
-                copy(ring, step + 1).start()
-    for step in range(6):
-        for ring in rings:
-            copy(ring, step).wait_send()
+        trunk.each(lambda ring: trunk.advance(ring, step))
+    color.drain()
+    trunk.drain()
 
 
 def communicate(kernel, name, number, args, specs, shapes, scratch):
@@ -688,7 +767,7 @@
         out_specs=jax.tree.map(lambda _: VMEM, shapes),
         scratch_shapes=scratch,
         compiler_params=pltpu.CompilerParams(
-            collective_id=number, has_side_effects=True, vmem_limit_bytes=16 * 1024 * 1024
+            collective_id=number, has_side_effects=True, vmem_limit_bytes=(32 if number == 2 else 16) * 1024 * 1024
         ),
         cost_estimate=pl.CostEstimate(flops=10**10, bytes_accessed=10**6, transcendentals=0),
     )(*args)
@@ -718,12 +797,20 @@
     )
 
 
-def run_total(packed):
+def run_trunk(color_grads, dz, trunk, saved):
+    f32, bf = jnp.float32, jnp.bfloat16
+    rows_a, rows_b = A_ROWS // 16, (G_ROWS - A_ROWS) // 16
     return communicate(
-        total_kernel, "total_gradients", 2, (packed,), [VMEM],
-        jax.ShapeDtypeStruct((G_ROWS, 256), jnp.float32),
-        [pltpu.VMEM((4, 3, CHUNK, 256), jnp.float32), pltpu.VMEM((4, 2, CHUNK, 256), jnp.float32)]
-        + [pltpu.SemaphoreType.DMA((4, 6))] * 2,
+        trunk_kernel, "trunk_and_total", 2,
+        (color_grads, dz, trunk, jnp.asarray(POS_SELECT, bf), saved), [VMEM, VMEM, VMEM, VMEM, ANY],
+        jax.ShapeDtypeStruct((G_ROWS, 256), f32),
+        [pltpu.VMEM((HID, HID), bf), pltpu.VMEM((HID, HID), bf), pltpu.VMEM((HID, 2 * LANES), bf),
+         pltpu.VMEM((HID, 2 * LANES), bf), pltpu.VMEM((G_ROWS - A_ROWS, 256), f32),
+         pltpu.VMEM((HID, PC), f32), pltpu.VMEM((DEEP, R_H3, 2 * LANES), bf),
+         pltpu.SemaphoreType.DMA((DEEP, len(LOW))),
+         pltpu.VMEM((4, 3, rows_a, 256), f32), pltpu.VMEM((4, 2, rows_a, 256), f32),
+         pltpu.VMEM((4, 3, rows_b, 256), f32), pltpu.VMEM((4, 2, rows_b, 256), f32)]
+        + [pltpu.SemaphoreType.DMA((4, 6))] * 4,
     )
 
 
@@ -742,11 +829,11 @@
         view_weight.transpose(0, 2, 1), code, radiance_weight, code_table,
     )
     colors, cot = run_blend(ids, part, color_grad)
-    packed = run_backward(
-        live, center, rays, cot, saved, raycode, small, trunk_weight, density_weight,
-        feature_weight, code, radiance_weight,
-    )
-    return run_unpack(run_total(packed), colors)
+    color_grads, dz = run_backward(
+        live, center, rays, cot, saved, raycode, small, density_weight, feature_weight, code,
+        radiance_weight,
+    )
+    return run_unpack(run_trunk(color_grads, dz, trunk_weight, saved), colors)
 
 
 def solution(mesh):

time: 109 us -> 121 us (1.11)
  the two profiles are of different devices: /device:TPU:1 before, /device:TPU:0 now
where the time goes in v1:
time: 121 us; the launch traced here: 120 us
  Pallas kernels  115 us (95%)
  local copies, waits for them, and re-layouts  2.82 us (2%)
    pallas_call x3, Pallas kernels, communicate(): pl.pallas_call(kernel, name=name, out_shape=shapes, in_specs=specs, out_s...  87.1 us
    pallas_call x1, Pallas kernels, run_forward(): pl.pallas_call(forward_kernel, name='forward_tiles', out_shape=(jax.Shape...  18.2 us
    pallas_call x1, Pallas kernels, run_backward(): pl.pallas_call(backward_kernel, name='backward_tiles', out_shape=(jax.Sha...  8.71 us
    unnamed x34, local copies, waits for them, and re-layouts  2.82 us

profile of v1, /device:TPU:0, one launch (start us, length us, event | category | flops | bytes accessed | tf_op | source)
XLA Modules:
  0.0 119.7 jit_solution(5917469709386861773)
XLA Ops:
  0.6 0.0 copy-start.5
  0.7 0.7 copy-done.5
  1.4 0.0 copy-start.6
  1.4 0.7 copy-done.6
  2.1 0.0 copy-start.10
  2.1 0.7 copy-done.10
  2.7 0.0 copy-start.11
  2.7 0.7 copy-done.11
  3.4 0.0 copy-start
  3.4 0.0 copy-start.1
  3.4 0.0 copy-start.2
  3.4 0.0 copy-start.3
  3.4 0.0 copy-start.4
  3.4 0.0 copy-start.8
  3.5 0.0 copy-start.9
  3.5 0.0 copy-start.13
  3.5 0.0 copy-start.14
  3.5 0.0 copy-start.15
  3.5 0.0 copy-start.16
  3.5 14.1 %scatter_rays.1.rays_ref = f32[32,8,128]{2,1,0:T(8,128)S(1)} custom-call(s32[3,5]{1,0:T(4,128)S(1)} %bitcast.15, f32[3,640]{1,0:T(4,128)S(1)} %copy-done.5, f32[3,640]{1,0:T(4,128)S(1)} %copy-done.6, s32[5,128]{1,0:T(8,128)S(1)} %bitcast.14), custom_call_target="tpu_custom_call" | custom-call | flops 10000000000 | bytes 1000000 | tf_op jit(solution)/shard_map/scatter_rays/pallas_call | solution.py:762
  17.6 0.7 fusion.live_ref
  18.3 0.0 copy-done
  18.3 0.0 copy-done.1
  18.3 0.0 copy-done.2
  18.3 0.0 copy-done.3
  18.3 0.0 copy-done.4
  18.3 0.0 copy-done.8
  18.3 0.0 copy-done.9
  18.3 0.0 copy-done.13
  18.3 0.0 copy-done.14
  18.4 0.0 copy-done.15
  18.4 0.0 copy-done.16
  18.4 0.0 copy-start.7
  18.4 0.0 copy-start.12
  18.4 18.2 %forward_tiles.1 = (f32[32,4,128]{2,1,0:T(4,128)S(1)}, bf16[16,992,1024]{2,1,0:T(8,128)(2,1)}, bf16[16,80,256]{2,1,0:T(8,128)(2,1)S(1)}, f32[16,8,1024]{2,1,0:T(8,128)S(1)}) custom-call(s32[32]{0:T(128)S(1)} %fusion.live_ref, f32[1,3]{1,0:T(1,128)S(1)} %bitcast.17, f32[32,8,128]{2,1,0:T(8,128)S(1)} %scatter_rays.1.rays_ref, ...), custom_call_target="tpu_custom_call" | custom-call | flops 10000000000 | bytes 30000000 | tf_op jit(solution)/shard_map/forward_tiles/pallas_call | solution.py:468
  36.6 0.0 copy-done.7
  36.6 0.0 copy-done.12
  36.6 20.7 %blend_colors.1 = (f32[3,640]{1,0:T(4,128)S(1)}, f32[32,4,128]{2,1,0:T(4,128)S(1)}) custom-call(s32[3,5]{1,0:T(4,128)S(1)} %bitcast.16, f32[32,4,128]{2,1,0:T(4,128)S(1)} %get-tuple-element.26.part_ref, f32[3,640]{1,0:T(4,128)S(1)} %copy-done.7), custom_call_target="tpu_custom_call" | custom-call | flops 10000000000 | bytes 1000000 | tf_op jit(solution)/shard_map/blend_colors/pallas_call | solution.py:762
  57.4 8.7 %backward_tiles.1 = (f32[1280,256]{1,0:T(8,128)S(1)}, bf16[16,256,1024]{2,1,0:T(8,128)(2,1)S(1)}) custom-call(s32[32]{0:T(128)S(1)} %fusion.live_ref, f32[1,3]{1,0:T(1,128)S(1)} %bitcast.18, f32[32,8,128]{2,1,0:T(8,128)S(1)} %scatter_rays.1.rays_ref, f32[32,4,128]{2,1,0:T(4,128)S(1)} %get-tuple-element.27.cot_ref, ...), custom_call_target="tpu_custom_call" | custom-call | flops 10000000000 | bytes 10000000 | tf_op jit(solution)/shard_map/backward_tiles/pallas_call | solution.py:498
  66.1 52.2 %trunk_and_total.1.g_ref = f32[1920,256]{1,0:T(8,128)S(1)} custom-call(f32[1280,256]{1,0:T(8,128)S(1)} %get-tuple-element.31.ga_ref, bf16[16,256,1024]{2,1,0:T(8,128)(2,1)S(1)} %get-tuple-element.32.dz_ref, bf16[1,2,256,256]{3,2,1,0:T(8,128)(2,1)S(1)} %copy-done, bf16[63,96]{1,0:T(8,128)(2,1)S(1)} %copy-done.1, ...), custom_call_target="tpu_custom_call" | custom-call | flops 10000000000 | bytes 1000000 | tf_op jit(solution)/shard_map/trunk_and_total/pallas_call | solution.py:762
  118.3 1.4 %unpack_gradients.1 = (f32[3,640]{1,0:T(4,128)}, f32[63,1,256]{2,1,0:T(1,128)}, f32[1,2,256,256]{3,2,1,0:T(8,128)}, f32[1,256]{1,0:T(1,128)}, f32[1,128,256]{2,1...) custom-call(f32[1920,256]{1,0:T(8,128)S(1)} %trunk_and_total.1.g_ref, ...), custom_call_target="tpu_custom_call" | custom-call | tf_op jit(solution)/shard_map/unpack_gradients/pallas_call | solution.py:528
Async XLA Ops:
  0.6 0.7 copy-start.5
  1.4 0.7 copy-start.6
  2.1 0.7 copy-start.10
  2.7 0.7 copy-start.11
  3.4 14.8 %copy-start = (bf16[1,2,256,256]{3,2,1,0:T(8,128)(2,1)S(1)}, bf16[1,2,256,256]{3,2,1,0:T(8,128)(2,1)}, u32[]{:S(2)}) copy-start(bf16[1,2,256,256]{3,2,1,0:T(8,128)(2,1)} %trunk_ref.3) | copy-start | bytes 786436
  3.4 14.9 %copy-start.1 = (bf16[63,96]{1,0:T(8,128)(2,1)S(1)}, bf16[63,96]{1,0:T(8,128)(2,1)}, u32[]{:S(2)}) copy-start(bf16[63,96]{1,0:T(8,128)(2,1)} %constant.6.clone.pos_select_ref) | copy-start | bytes 36292
  3.4 14.9 %copy-start.2 = (bf16[1,32,8192]{2,1,0:T(8,128)(2,1)S(1)}, bf16[1,32,8192]{2,1,0:T(8,128)(2,1)}, u32[]{:S(2)}) copy-start(bf16[1,32,8192]{2,1,0:T(8,128)(2,1)} %table_ref.1) | copy-start | bytes 1572868
  3.4 14.9 %copy-start.3 = (bf16[1,128,256]{2,1,0:T(8,128)(2,1)S(1)}, bf16[1,128,256]{2,1,0:T(8,128)(2,1)}, u32[]{:S(2)}) copy-start(bf16[1,128,256]{2,1,0:T(8,128)(2,1)} %feature_ref.3) | copy-start | bytes 196612
  3.4 14.9 %copy-start.4 = (bf16[1,256,63]{1,2,0:T(8,128)(2,1)S(1)}, bf16[1,256,63]{1,2,0:T(8,128)(2,1)}, u32[]{:S(2)}) copy-start(bf16[1,256,63]{1,2,0:T(8,128)(2,1)} %param.24) | copy-start | bytes 96772
  3.4 14.9 %copy-start.8 = (bf16[1,128,27]{1,2,0:T(8,128)(2,1)S(1)}, bf16[1,128,27]{1,2,0:T(8,128)(2,1)}, u32[]{:S(2)}) copy-start(bf16[1,128,27]{1,2,0:T(8,128)(2,1)} %param.28) | copy-start | bytes 20740
  3.5 14.9 %copy-start.9 = (bf16[1,128,32]{1,2,0:T(8,128)(2,1)S(1)}, bf16[1,128,32]{1,2,0:T(8,128)(2,1)}, u32[]{:S(2)}) copy-start(bf16[1,128,32]{1,2,0:T(8,128)(2,1)} %param.29) | copy-start | bytes 24580
  3.5 14.9 %copy-start.13 = (bf16[1,256]{1,0:T(2,128)(2,1)S(1)}, bf16[1,256]{1,0:T(2,128)(2,1)}, u32[]{:S(2)}) copy-start(bf16[1,256]{1,0:T(2,128)(2,1)} %density_ref.3) | copy-start | bytes 1540
  3.5 14.9 %copy-start.14 = (bf16[1,3,128]{2,1,0:T(4,128)(2,1)S(1)}, bf16[1,3,128]{2,1,0:T(4,128)(2,1)}, u32[]{:S(2)}) copy-start(bf16[1,3,128]{2,1,0:T(4,128)(2,1)} %radiance_ref.3) | copy-start | bytes 2308
  3.5 14.9 %copy-start.15 = (f32[3,1]{0,1:T(1,128)S(1)}, f32[3,1]{0,1:T(1,128)}, u32[]{:S(2)}) copy-start(f32[3,1]{0,1:T(1,128)} %param.23) | copy-start | bytes 40
  3.5 14.9 %copy-start.16 = (bf16[27,48]{1,0:T(8,128)(2,1)S(1)}, bf16[27,48]{1,0:T(8,128)(2,1)}, u32[]{:S(2)}) copy-start(bf16[27,48]{1,0:T(8,128)(2,1)} %constant.7.clone.view_select_ref) | copy-start | bytes 7780
  18.4 18.2 %copy-start.7 = (f32[3,640]{1,0:T(4,128)S(1)}, f32[3,640]{1,0:T(4,128)}, u32[]{:S(2)}) copy-start(f32[3,640]{1,0:T(4,128)} %grad_ref.1) | copy-start | bytes 23044
  18.4 18.2 %copy-start.12 = (s32[5,3]{0,1:T(4,128)S(1)}, s32[5,3]{0,1:T(4,128)}, u32[]{:S(2)}) copy-start(s32[5,3]{0,1:T(4,128)} %param.21) | copy-start | bytes 184

commit v2 on v1

--- a/solution.py
+++ b/solution.py
@@ -209,7 +209,7 @@
     live_ref, center_ref, rays_ref, pos_ref, trunk_ref, density_ref, feature_ref, view_ref,
     code_ref, radiance_ref, table_ref, pos_select_ref, view_select_ref,
     part_ref, saved_ref, raycode_ref, small_ref,
-    wp, wfd, wray, wrad, tab, buf, slots, sem, blank_sem,
+    wp, wfd, wray, wrad, tab, buf, zeros, slots, sem, blank_sem,
 ):
     row = row_iota(8, 2 * TILE)
     c8 = center_rows(center_ref, row)
@@ -228,6 +228,16 @@
     pos_scale = jnp.where(row < 3, 1.0, 32.0)
     view_scale = jnp.where(row < 3, 1.0, 4.0)
     total, pairs = list_live(live_ref, slots)
+    zeros[...] = jnp.zeros_like(zeros)
+
+    def blank(j):
+        return pltpu.make_async_copy(zeros, saved_ref.at[j, :R_H3], blank_sem.at[j])
+
+    def begin_blank(j, carry):
+        blank(j).start()
+        return carry
+
+    lax.fori_loop(pairs, PAIRS, begin_blank, jnp.int32(0))
 
     def finish_pair(j):
         s0, s1 = slots[2 * j], slots[2 * j + 1]
@@ -296,20 +306,11 @@
         return carry
 
     lax.fori_loop(jnp.maximum(pairs - DEEP, 0), pairs, drain, jnp.int32(0))
-    buf[0, :R_H3, :] = jnp.zeros((R_H3, 2 * LANES), jnp.bfloat16)
-
-    def blank(j):
-        return pltpu.make_async_copy(buf.at[0, :R_H3], saved_ref.at[j, :R_H3], blank_sem.at[j])
-
-    def begin_blank(j, carry):
-        blank(j).start()
-        return carry
 
     def end_blank(j, carry):
         blank(j).wait()
         return carry
 
-    lax.fori_loop(pairs, PAIRS, begin_blank, jnp.int32(0))
     lax.fori_loop(pairs, PAIRS, end_blank, jnp.int32(0))
 
 
@@ -483,6 +484,7 @@
             pltpu.VMEM((8, CHID), bf),
             pltpu.VMEM((SLOTS * E, LO), bf),
             pltpu.VMEM((DEEP, R_END, 2 * LANES), bf),
+            pltpu.VMEM((R_H3, 2 * LANES), bf),
             pltpu.SMEM((SLOTS + 1,), jnp.int32),
             pltpu.SemaphoreType.DMA((DEEP, len(ALL))),
             pltpu.SemaphoreType.DMA((PAIRS,)),
@@ -750,9 +752,9 @@
         lax.fori_loop(0, 4, both, 0)
     gb[2 * HID : 2 * HID + 63, :] = pick(g_pos[...], pos_select_ref[...])
     trunk.begin()
-    for step in (4, 5):
-        color.each(lambda ring: color.advance(ring, step))
     for step in range(6):
+        if step < 2:
+            color.each(lambda ring: color.advance(ring, 4 + step))
         trunk.each(lambda ring: trunk.advance(ring, step))
     color.drain()
     trunk.drain()

time: 121 us -> 114 us (0.942)
  Pallas kernels: 115 us -> 108 us
    pallas_call x1, Pallas kernels: 18.2 us -> 12.4 us  [run_forward(): pl.pallas_call(forward_kernel, name='forward_tiles', out_shape=(jax.Shape...]
where the time goes in v2:
time: 114 us; the launch traced here: 112 us
  Pallas kernels  108 us (95%)
  local copies, waits for them, and re-layouts  2.82 us (2%)
    pallas_call x3, Pallas kernels, communicate(): pl.pallas_call(kernel, name=name, out_shape=shapes, in_specs=specs, out_s...  86.6 us
    pallas_call x1, Pallas kernels, run_forward(): pl.pallas_call(forward_kernel, name='forward_tiles', out_shape=(jax.Shape...  12.4 us
    pallas_call x1, Pallas kernels, run_backward(): pl.pallas_call(backward_kernel, name='backward_tiles', out_shape=(jax.Sha...  7.75 us
    unnamed x34, local copies, waits for them, and re-layouts  2.82 us

profile of v2, /device:TPU:0, one launch (start us, length us, event | category | flops | bytes accessed | tf_op | source)
XLA Modules:
  0.0 112.5 jit_solution(8910048765259745974)
XLA Ops:
  0.6 0.0 copy-start.5
  0.7 0.7 copy-done.5
  1.4 0.0 copy-start.6
  1.4 0.7 copy-done.6
  2.1 0.0 copy-start.10
  2.1 0.7 copy-done.10
  2.7 0.0 copy-start.11
  2.7 0.7 copy-done.11
  3.4 0.0 copy-start
  3.4 0.0 copy-start.1
  3.4 0.0 copy-start.2
  3.4 0.0 copy-start.3
  3.4 0.0 copy-start.4
  3.4 0.0 copy-start.8
  3.5 0.0 copy-start.9
  3.5 0.0 copy-start.13
  3.5 0.0 copy-start.14
  3.5 0.0 copy-start.15
  3.5 0.0 copy-start.16
  3.5 14.1 %scatter_rays.1.rays_ref = f32[32,8,128]{2,1,0:T(8,128)S(1)} custom-call(s32[3,5]{1,0:T(4,128)S(1)} %bitcast.15, f32[3,640]{1,0:T(4,128)S(1)} %copy-done.5, f32[3,640]{1,0:T(4,128)S(1)} %copy-done.6, s32[5,128]{1,0:T(8,128)S(1)} %bitcast.14), custom_call_target="tpu_custom_call" | custom-call | flops 10000000000 | bytes 1000000 | tf_op jit(solution)/shard_map/scatter_rays/pallas_call | solution.py:764
  17.6 0.7 fusion.live_ref
  18.3 0.0 copy-done
  18.3 0.0 copy-done.1
  18.3 0.0 copy-done.2
  18.3 0.0 copy-done.3
  18.3 0.0 copy-done.4
  18.3 0.0 copy-done.8
  18.3 0.0 copy-done.9
  18.3 0.0 copy-done.13
  18.3 0.0 copy-done.14
  18.4 0.0 copy-done.15
  18.4 0.0 copy-done.16
  18.4 0.0 copy-start.7
  18.4 0.0 copy-start.12
  18.4 12.4 %forward_tiles.1 = (f32[32,4,128]{2,1,0:T(4,128)S(1)}, bf16[16,992,1024]{2,1,0:T(8,128)(2,1)}, bf16[16,80,256]{2,1,0:T(8,128)(2,1)S(1)}, f32[16,8,1024]{2,1,0:T(8,128)S(1)}) custom-call(s32[32]{0:T(128)S(1)} %fusion.live_ref, f32[1,3]{1,0:T(1,128)S(1)} %bitcast.17, f32[32,8,128]{2,1,0:T(8,128)S(1)} %scatter_rays.1.rays_ref, ...), custom_call_target="tpu_custom_call" | custom-call | flops 10000000000 | bytes 30000000 | tf_op jit(solution)/shard_map/forward_tiles/pallas_call | solution.py:469
  30.8 0.0 copy-done.7
  30.8 0.0 copy-done.12
  30.8 24.5 %blend_colors.1 = (f32[3,640]{1,0:T(4,128)S(1)}, f32[32,4,128]{2,1,0:T(4,128)S(1)}) custom-call(s32[3,5]{1,0:T(4,128)S(1)} %bitcast.16, f32[32,4,128]{2,1,0:T(4,128)S(1)} %get-tuple-element.26.part_ref, f32[3,640]{1,0:T(4,128)S(1)} %copy-done.7), custom_call_target="tpu_custom_call" | custom-call | flops 10000000000 | bytes 1000000 | tf_op jit(solution)/shard_map/blend_colors/pallas_call | solution.py:764
  55.3 7.8 %backward_tiles.1 = (f32[1280,256]{1,0:T(8,128)S(1)}, bf16[16,256,1024]{2,1,0:T(8,128)(2,1)S(1)}) custom-call(s32[32]{0:T(128)S(1)} %fusion.live_ref, f32[1,3]{1,0:T(1,128)S(1)} %bitcast.18, f32[32,8,128]{2,1,0:T(8,128)S(1)} %scatter_rays.1.rays_ref, f32[32,4,128]{2,1,0:T(4,128)S(1)} %get-tuple-element.27.cot_ref, ...), custom_call_target="tpu_custom_call" | custom-call | flops 10000000000 | bytes 10000000 | tf_op jit(solution)/shard_map/backward_tiles/pallas_call | solution.py:500
  63.1 48.0 %trunk_and_total.1.g_ref = f32[1920,256]{1,0:T(8,128)S(1)} custom-call(f32[1280,256]{1,0:T(8,128)S(1)} %get-tuple-element.31.ga_ref, bf16[16,256,1024]{2,1,0:T(8,128)(2,1)S(1)} %get-tuple-element.32.dz_ref, bf16[1,2,256,256]{3,2,1,0:T(8,128)(2,1)S(1)} %copy-done, bf16[63,96]{1,0:T(8,128)(2,1)S(1)} %copy-done.1, ...), custom_call_target="tpu_custom_call" | custom-call | flops 10000000000 | bytes 1000000 | tf_op jit(solution)/shard_map/trunk_and_total/pallas_call | solution.py:764
  111.1 1.4 %unpack_gradients.1 = (f32[3,640]{1,0:T(4,128)}, f32[63,1,256]{2,1,0:T(1,128)}, f32[1,2,256,256]{3,2,1,0:T(8,128)}, f32[1,256]{1,0:T(1,128)}, f32[1,128,256]{2,1...) custom-call(f32[1920,256]{1,0:T(8,128)S(1)} %trunk_and_total.1.g_ref, ...), custom_call_target="tpu_custom_call" | custom-call | tf_op jit(solution)/shard_map/unpack_gradients/pallas_call | solution.py:530
Async XLA Ops:
  0.6 0.7 copy-start.5
  1.4 0.7 copy-start.6
  2.1 0.7 copy-start.10
  2.7 0.7 copy-start.11
  3.4 14.8 %copy-start = (bf16[1,2,256,256]{3,2,1,0:T(8,128)(2,1)S(1)}, bf16[1,2,256,256]{3,2,1,0:T(8,128)(2,1)}, u32[]{:S(2)}) copy-start(bf16[1,2,256,256]{3,2,1,0:T(8,128)(2,1)} %trunk_ref.3) | copy-start | bytes 786436
  3.4 14.9 %copy-start.1 = (bf16[63,96]{1,0:T(8,128)(2,1)S(1)}, bf16[63,96]{1,0:T(8,128)(2,1)}, u32[]{:S(2)}) copy-start(bf16[63,96]{1,0:T(8,128)(2,1)} %constant.6.clone.pos_select_ref) | copy-start | bytes 36292
  3.4 14.9 %copy-start.2 = (bf16[1,32,8192]{2,1,0:T(8,128)(2,1)S(1)}, bf16[1,32,8192]{2,1,0:T(8,128)(2,1)}, u32[]{:S(2)}) copy-start(bf16[1,32,8192]{2,1,0:T(8,128)(2,1)} %table_ref.1) | copy-start | bytes 1572868
  3.4 14.9 %copy-start.3 = (bf16[1,128,256]{2,1,0:T(8,128)(2,1)S(1)}, bf16[1,128,256]{2,1,0:T(8,128)(2,1)}, u32[]{:S(2)}) copy-start(bf16[1,128,256]{2,1,0:T(8,128)(2,1)} %feature_ref.3) | copy-start | bytes 196612
  3.4 14.9 %copy-start.4 = (bf16[1,256,63]{1,2,0:T(8,128)(2,1)S(1)}, bf16[1,256,63]{1,2,0:T(8,128)(2,1)}, u32[]{:S(2)}) copy-start(bf16[1,256,63]{1,2,0:T(8,128)(2,1)} %param.24) | copy-start | bytes 96772
  3.4 14.9 %copy-start.8 = (bf16[1,128,27]{1,2,0:T(8,128)(2,1)S(1)}, bf16[1,128,27]{1,2,0:T(8,128)(2,1)}, u32[]{:S(2)}) copy-start(bf16[1,128,27]{1,2,0:T(8,128)(2,1)} %param.28) | copy-start | bytes 20740
  3.5 14.9 %copy-start.9 = (bf16[1,128,32]{1,2,0:T(8,128)(2,1)S(1)}, bf16[1,128,32]{1,2,0:T(8,128)(2,1)}, u32[]{:S(2)}) copy-start(bf16[1,128,32]{1,2,0:T(8,128)(2,1)} %param.29) | copy-start | bytes 24580
  3.5 14.9 %copy-start.13 = (bf16[1,256]{1,0:T(2,128)(2,1)S(1)}, bf16[1,256]{1,0:T(2,128)(2,1)}, u32[]{:S(2)}) copy-start(bf16[1,256]{1,0:T(2,128)(2,1)} %density_ref.3) | copy-start | bytes 1540
  3.5 14.9 %copy-start.14 = (bf16[1,3,128]{2,1,0:T(4,128)(2,1)S(1)}, bf16[1,3,128]{2,1,0:T(4,128)(2,1)}, u32[]{:S(2)}) copy-start(bf16[1,3,128]{2,1,0:T(4,128)(2,1)} %radiance_ref.3) | copy-start | bytes 2308
  3.5 14.9 %copy-start.15 = (f32[3,1]{0,1:T(1,128)S(1)}, f32[3,1]{0,1:T(1,128)}, u32[]{:S(2)}) copy-start(f32[3,1]{0,1:T(1,128)} %param.23) | copy-start | bytes 40
  3.5 14.9 %copy-start.16 = (bf16[27,48]{1,0:T(8,128)(2,1)S(1)}, bf16[27,48]{1,0:T(8,128)(2,1)}, u32[]{:S(2)}) copy-start(bf16[27,48]{1,0:T(8,128)(2,1)} %constant.7.clone.view_select_ref) | copy-start | bytes 7780
  18.4 12.5 %copy-start.7 = (f32[3,640]{1,0:T(4,128)S(1)}, f32[3,640]{1,0:T(4,128)}, u32[]{:S(2)}) copy-start(f32[3,640]{1,0:T(4,128)} %grad_ref.1) | copy-start | bytes 23044
  18.4 12.4 %copy-start.12 = (s32[5,3]{0,1:T(4,128)S(1)}, s32[5,3]{0,1:T(4,128)}, u32[]{:S(2)}) copy-start(s32[5,3]{0,1:T(4,128)} %param.21) | copy-start | bytes 184
